TPU v7x, 32 devices: a whole 2x2x4 slice. The times are simulated.
32 devices in a mesh: peer: 8 (over y, x, core), zero: 4 (over z).
Axes of the slice: x: 2, y: 2, z: 4, core: 2. Of those that a mesh axis runs over, the one named last changes fastest.
Arguments:
- tokens: bfloat16 [8, 2048, 1024], P('peer', 'zero'), may hold values from -6 to 6
- out_grad: bfloat16 [8, 2048, 1024], P('peer', 'zero'), may hold values from -6 to 6
- step: int32 [1], replicated, may hold values from 0 to 3999
- up_param: float32 [8, 1024, 2048], P('peer', 'zero'), may hold values from -0.2 to 0.2
- down_param: float32 [8, 2048, 1024], P('peer', 'zero'), may hold values from -0.2 to 0.2
- up_first: float32 [8, 1024, 2048], P('peer', 'zero'), may hold values from -27.1529 to 27.1529
- down_first: float32 [8, 2048, 1024], P('peer', 'zero'), may hold values from -27.1529 to 27.1529
- up_second: float32 [8, 1024, 2048], P('peer', 'zero'), may hold values from 0.8192 to 819.2
- down_second: float32 [8, 2048, 1024], P('peer', 'zero'), may hold values from 0.8192 to 819.2
Outputs:
- new_up: float32 [8, 1024, 2048], P('peer', 'zero')
- new_down: float32 [8, 2048, 1024], P('peer', 'zero')
- new_up_first: float32 [8, 1024, 2048], P('peer', 'zero')
- new_down_first: float32 [8, 2048, 1024], P('peer', 'zero')
- new_up_second: float32 [8, 1024, 2048], P('peer', 'zero')
- new_down_second: float32 [8, 2048, 1024], P('peer', 'zero')
All inputs are finite; a program needn't handle non-finite values.
Results may differ from a plain program's by a relative error of at most 0.0065.
Values may be sent and summed in bfloat16 or wider, within the bound.
A program may use at most 128 MiB of HBM per device.

v0:
```python
from functools import partial
import jax
import jax.numpy as jnp
from jax import lax
from jax.sharding import PartitionSpec as P


def passed_along(array, axis, by):
    size = lax.axis_size(axis)
    return lax.ppermute(array, axis, [(i, (i + by) % size) for i in range(size)])


def gelu_tanh(values):
    return (
        0.5
        * values
        * (1.0 + jnp.tanh(0.7978845608 * (values + 0.044715 * values * values * values)))
    )


def adam_update(param, first, second, grad, first_fix, second_fix):
    first_new = 0.9 * first + 0.1 * grad
    second_new = 0.999 * second + 0.001 * grad * grad
    local = param - 0.01 * (first_new / first_fix) / (jnp.sqrt(second_new / second_fix) + 1e-08)
    return (local, first_new, second_new)


def across_rows(left, right):
    return lax.dot_general(
        left, right, (((0,), (0,)), ((), ())), preferred_element_type=jnp.float32
    )


def from_partner(pair, by):
    return passed_along(pair, "peer", -by)


def body(
    tokens, out_grad, step, up_param, down_param, up_first, down_first, up_second, down_second
):
    grad_rows = out_grad[0]
    widened = tokens[0].astype(jnp.float32)
    center = jnp.mean(widened, axis=1, keepdims=True)
    spread = jnp.mean((widened - center) * (widened - center), axis=1, keepdims=True)
    normed = ((widened - center) * lax.rsqrt(spread + 1e-05)).astype(jnp.bfloat16)
    up_low = up_param[0].astype(jnp.bfloat16)
    down_low = down_param[0].astype(jnp.bfloat16)
    columns = normed
    pre = jnp.dot(
        columns,
        lax.all_gather(up_low, "zero", axis=0, tiled=True),
        preferred_element_type=jnp.float32,
    )
    active, backward = jax.vjp(gelu_tanh, pre)
    act_grad = lax.dot_general(
        grad_rows,
        lax.all_gather(down_low, "zero", axis=0, tiled=True),
        (((1,), (1,)), ((), ())),
        preferred_element_type=jnp.float32,
    )
    act = active.astype(jnp.bfloat16)
    pre_grad = backward(act_grad)[0].astype(jnp.bfloat16)
    columns = normed
    up_grad = lax.psum_scatter(
        across_rows(columns, pre_grad).astype(jnp.bfloat16), "zero", scatter_dimension=0, tiled=True
    ).astype(jnp.float32)
    columns = act
    down_grad = lax.psum_scatter(
        across_rows(columns, grad_rows).astype(jnp.bfloat16),
        "zero",
        scatter_dimension=0,
        tiled=True,
    ).astype(jnp.float32)
    count = (step[0] + 1).astype(jnp.float32)
    first_fix = 1.0 - jnp.power(jnp.float32(0.9), count)
    second_fix = 1.0 - jnp.power(jnp.float32(0.999), count)
    up_local, up_first_new, up_second_new = adam_update(
        up_param[0], up_first[0], up_second[0], up_grad, first_fix, second_fix
    )
    down_local, down_first_new, down_second_new = adam_update(
        down_param[0], down_first[0], down_second[0], down_grad, first_fix, second_fix
    )
    levels = lax.axis_size("peer").bit_length() - 1
    branches = [partial(from_partner, by=2**level) for level in range(levels)]
    up_other, down_other = lax.switch(step[0] % levels, branches, (up_local, down_local))
    new_up = 0.5 * (up_local + up_other)
    new_down = 0.5 * (down_local + down_other)
    return (
        new_up[None],
        new_down[None],
        up_first_new[None],
        down_first_new[None],
        up_second_new[None],
        down_second_new[None],
    )


def solution(mesh):
    in_specs = (
        P("peer", "zero", None),
        P("peer", "zero", None),
        P(),
        P("peer", "zero", None),
        P("peer", "zero", None),
        P("peer", "zero", None),
        P("peer", "zero", None),
        P("peer", "zero", None),
        P("peer", "zero", None),
    )
    out_specs = (
        P("peer", "zero", None),
        P("peer", "zero", None),
        P("peer", "zero", None),
        P("peer", "zero", None),
        P("peer", "zero", None),
        P("peer", "zero", None),
    )
    return jax.shard_map(body, mesh=mesh, in_specs=in_specs, out_specs=out_specs, check_vma=False)
```

profile of v0, /device:TPU:0, one launch (start us, length us, event | category | flops | bytes accessed | tf_op | source)
XLA Modules:
  0.0 454.6 jit_solution(11228907826659699742)
XLA Ops:
  7.2 0.0 copy-start
  7.2 0.0 copy-start.1
  7.2 0.0 all-gather.3.cloned.1.call-start
  7.2 2.9 bitcast_convert_fusion.1
  10.1 0.0 all-gather.3.cloned.1.call-update
  10.1 0.0 all-gather.5.cloned.1.call-start
  10.2 0.0 copy-done.1
  10.2 1.1 bitcast_convert_fusion
  11.3 0.0 copy-start.2
  11.3 0.0 all-gather.5.cloned.1.call-update
  11.3 0.0 reduce-scatter.3.cloned.1.call-start
  11.4 1.5 convert_reduce_fusion
  12.9 0.0 copy-done.2
  12.9 0.4 fusion.9
  13.3 80.4 %all-gather.3.cloned.1.call-done = bf16[1024,2048]{1,0:T(8,128)(2,1)} async-done(((bf16[256,2048]{1,0:T(8,128)(2,1)}), bf16[1024,2048]{1,0:T(8,128)(2,1)}) %all-gather.3.cloned.1.call-update) | async-done | bytes 4194320 | tf_op jit(solution)/shard_map/all_gather | solution.py:51
  93.7 6.6 %fusion.40 = f32[512,2048]{1,0:T(8,128)} fusion(bf16[1024,2048]{1,0:T(8,128)(2,1)} %all-gather.3.cloned.1.call-done, bf16[1,512,1024]{2,1,0:T(8,128)(2,1)S(1)} %copy-done.2, f32[512]{0:T(512)S(1)} %add_rsqrt_fusion, f32[512]{0:T(512)S(1)} %broadcast_multiply_fusion), kind=kOutput, calls=%fused_computation.55 | convolution fusion | flops 2149580800 | bytes 9441280 | tf_op jit(solution)/shard_map/dot_general | solution.py:49
  100.3 74.8 %all-gather.5.cloned.1.call-done = bf16[2048,1024]{1,0:T(8,128)(2,1)} async-done(((bf16[512,1024]{1,0:T(8,128)(2,1)}), bf16[2048,1024]{1,0:T(8,128)(2,1)}) %all-gather.5.cloned.1.call-update) | async-done | bytes 4194320 | tf_op jit(solution)/shard_map/all_gather | solution.py:57
  175.1 0.0 copy-done
  175.1 11.0 %convolution_convert_fusion.1 = bf16[1024,2048]{1,0:T(8,128)(2,1)} fusion(f32[512,2048]{1,0:T(8,128)} %fusion.40, bf16[2048,1024]{1,0:T(8,128)(2,1)} %all-gather.5.cloned.1.call-done, bf16[1,512,1024]{2,1,0:T(8,128)(2,1)S(1)} %copy-done, bf16[1,512,1024]{2,1,0:T(8,128)(2,1)S(1)} %copy-done.2, f32[512]{0:T(512)S(1)} %add_rsqrt_fusion, ...), kind=kOutput, calls=%fused_computation.12 | convolution fusion | flops 4324327424 | bytes 14684160 | tf_op jit(solution)/shard_map/dot_general | solution.py:29
  186.2 0.0 reduce-scatter.3.cloned.1.call-update
  186.2 0.2 reduce-scatter.5.cloned.1.call-start
  186.4 7.1 %convolution_convert_fusion = bf16[2048,1024]{1,0:T(8,128)(2,1)} fusion(f32[512,2048]{1,0:T(8,128)} %fusion.40, bf16[1,512,1024]{2,1,0:T(8,128)(2,1)S(1)} %copy-done), kind=kOutput, calls=%fused_computation.11 | convolution fusion | flops 2159017984 | bytes 9437184 | tf_op jit(solution)/shard_map/dot_general | solution.py:29
  193.5 0.0 reduce-scatter.5.cloned.1.call-update
  194.3 67.3 %reduce-scatter.3.cloned.1.call-done = bf16[256,2048]{1,0:T(8,128)(2,1)} async-done(((bf16[1024,2048]{1,0:T(8,128)(2,1)}), bf16[256,2048]{1,0:T(8,128)(2,1)}) %reduce-scatter.3.cloned.1.call-update) | async-done | bytes 1048592 | tf_op jit(solution)/shard_map/reduce_scatter | solution.py:64
  261.6 6.7 %fusion.23 = (f32[1,256,2048]{2,1,0:T(8,128)}, f32[256,2048]{1,0:T(8,128)S(1)}, f32[1,256,2048]{2,1,0:T(8,128)}) fusion(bf16[256,2048]{1,0:T(8,128)(2,1)} %reduce-scatter.3.cloned.1.call-done, f32[1,256,2048]{2,1,0:T(8,128)} %param.19, f32[]{:T(128)} %bitcast.7, f32[]{:T(128)} %bitcast.5, f32[1,256,2048]{2,1,0:T(8,128)} %param.17, f32[1,256,2048]{2,1,0:T(8,128)} %param.15), kind=kLoop, calls=%fused_computation.41 | loop fusion | flops 7340032 | bytes 13631496 | tf_op jit(solution)/shard_map/broadcast_in_dim | solution.py:93
  268.3 72.8 %reduce-scatter.5.cloned.1.call-done = bf16[512,1024]{1,0:T(8,128)(2,1)} async-done(((bf16[2048,1024]{1,0:T(8,128)(2,1)}), bf16[512,1024]{1,0:T(8,128)(2,1)}) %reduce-scatter.5.cloned.1.call-update) | async-done | bytes 1048592 | tf_op jit(solution)/shard_map/reduce_scatter | solution.py:68
  341.1 7.5 %fusion.22 = (f32[1,512,1024]{2,1,0:T(8,128)}, f32[512,1024]{1,0:T(8,128)}, f32[1,512,1024]{2,1,0:T(8,128)}) fusion(bf16[512,1024]{1,0:T(8,128)(2,1)} %reduce-scatter.5.cloned.1.call-done, f32[1,512,1024]{2,1,0:T(8,128)} %param.20, f32[]{:T(128)} %bitcast.7, f32[]{:T(128)} %bitcast.5, f32[1,512,1024]{2,1,0:T(8,128)} %param.18, f32[1,512,1024]{2,1,0:T(8,128)} %param.16), kind=kLoop, calls=%fused_computation.40 | loop fusion | flops 7340032 | bytes 13631496 | tf_op jit(solution)/shard_map/broadcast_in_dim | solution.py:94
  348.6 92.1 %conditional.1 = (f32[256,2048]{1,0:T(8,128)}, f32[512,1024]{1,0:T(8,128)}) conditional(s32[]{:T(128)} %clamp.3, (f32[256,2048]{1,0:T(8,128)S(1)}, f32[512,1024]{1,0:T(8,128)}) %tuple.20, (f32[256,2048]{1,0:T(8,128)S(1)}, f32[512,1024]{1,0:T(8,128)}) %tuple.20, (f32[256,2048]{1,0:T(8,128)S(1)}, f32[512,1024]{1,0:T(8,128)}) %tuple.20), branch_computations={%region_4.5_spmd, %region_5.6_spmd, %region_6.7_spmd} | conditional | bytes 16777312 | solution.py:85
  348.6 2.4 collective-permute-start.2
  351.0 0.6 collective-permute-start.3
  351.5 45.7 %collective-permute-done.2 = f32[256,2048]{1,0:T(8,128)} collective-permute-done((f32[256,2048]{1,0:T(8,128)S(1)}, f32[256,2048]{1,0:T(8,128)}, u32[]{:S(2)}, u32[]{:S(2)}) %collective-permute-start.2) | collective-permute-done | bytes 2097184 | tf_op jit(solution)/shard_map/cond/branch_1_fun/ppermute | solution.py:10
  397.2 43.5 %collective-permute-done.3 = f32[512,1024]{1,0:T(8,128)} collective-permute-done((f32[512,1024]{1,0:T(8,128)}, f32[512,1024]{1,0:T(8,128)}, u32[]{:S(2)}, u32[]{:S(2)}) %collective-permute-start.3) | collective-permute-done | bytes 2097184 | tf_op jit(solution)/shard_map/cond/branch_1_fun/ppermute | solution.py:10
  440.7 3.2 multiply_bitcast_fusion.1
  443.9 4.2 multiply_bitcast_fusion
  (2 shorter events, 0.0 us)
Async XLA Ops:
  7.2 168.0 %copy-start = (bf16[1,512,1024]{2,1,0:T(8,128)(2,1)S(1)}, bf16[1,512,1024]{2,1,0:T(8,128)(2,1)}, u32[]{:S(2)}) copy-start(bf16[1,512,1024]{2,1,0:T(8,128)(2,1)} %param.13) | copy-start | bytes 3145732
  7.2 3.0 copy-start.1
  7.2 86.6 %all-gather.3.cloned.1.call-start = ((), (), s32[]{:S(2)}) async-start(), calls=%async_computation.2 | async-start | bytes 5242880 | tf_op jit(solution)/shard_map/all_gather | solution.py:51
  10.1 165.0 %all-gather.5.cloned.1.call-start = ((), (), s32[]{:S(2)}) async-start(), calls=%async_computation.3 | async-start | bytes 5242880 | tf_op jit(solution)/shard_map/all_gather | solution.py:57
  11.3 1.6 copy-start.2
  11.3 250.3 %reduce-scatter.3.cloned.1.call-start = ((), (), s32[]{:S(2)}) async-start(), calls=%async_computation.4 | async-start | bytes 5242880 | tf_op jit(solution)/shard_map/reduce_scatter | solution.py:64
  186.2 154.9 %reduce-scatter.5.cloned.1.call-start = ((), (), s32[]{:S(2)}) async-start(), calls=%async_computation.5 | async-start | bytes 5242880 | tf_op jit(solution)/shard_map/reduce_scatter | solution.py:68
  348.6 48.6 %collective-permute-start.2 = (f32[256,2048]{1,0:T(8,128)S(1)}, f32[256,2048]{1,0:T(8,128)}, u32[]{:S(2)}, u32[]{:S(2)}) collective-permute-start(f32[256,2048]{1,0:T(8,128)S(1)} %get-tuple-element.14), channel_id=1, source_target_pairs={{0,24},{4,28},{8,0},{12,4},{16,8},{20,12},{24,16},{28,20},{1,25},{... | collective-permute-start | bytes 6291464 | tf_op jit(solution)/shard_map/cond/branch_1_fun/ppermute | solution.py:10
  351.0 89.7 %collective-permute-start.3 = (f32[512,1024]{1,0:T(8,128)}, f32[512,1024]{1,0:T(8,128)}, u32[]{:S(2)}, u32[]{:S(2)}) collective-permute-start(f32[512,1024]{1,0:T(8,128)} %get-tuple-element.15), channel_id=1, source_target_pairs={{0,24},{4,28},{8,0},{12,4},{16,8},{20,12},{24,16},{28,20},{1,25},{... | collective-permute-start | bytes 6291464 | tf_op jit(solution)/shard_map/cond/branch_1_fun/ppermute | solution.py:10
Sparse Core Ops, SparseCore 0:
  10.2 83.4 all-gather.2
  95.9 79.2 all-gather.4
  186.3 75.2 reduce-scatter.2
  263.8 77.2 reduce-scatter.4
where the time goes:
time: 455 us
  waiting for transfers between devices  385 us (85%)
  other arithmetic  27.5 us (6%)
  matrix products  24.7 us (5%)
  between operations  14.5 us (3%)
    ppermute x2, waiting for transfers between devices, passed_along(): lax.ppermute(array, axis, [(i, (i + by) % size) for i in range(size)])  89.2 us
    all_gather x1, waiting for transfers between devices, body(): lax.all_gather(up_low, 'zero', axis=0, tiled=True)  80.4 us
    all_gather x1, waiting for transfers between devices, body(): lax.all_gather(down_low, 'zero', axis=0, tiled=True)  74.8 us
    reduce_scatter x1, waiting for transfers between devices, body(): lax.psum_scatter(across_rows(columns, grad_rows).astype(jnp.bfloat16), 'z...  72.8 us
    reduce_scatter x1, waiting for transfers between devices, body(): lax.psum_scatter(across_rows(columns, pre_grad).astype(jnp.bfloat16), 'ze...  67.3 us
    dot_general x2, matrix products, across_rows(): lax.dot_general(left, right, (((0,), (0,)), ((), ())), preferred_element_...  18.1 us
  transfers between devices with their start and end apart: 6, of which 6 were waited for; matrix products, arithmetic and copies ran while one was open for 5% of the time, Pallas kernels for 0%

commit v1 on v0

--- a/solution.py
+++ b/solution.py
@@ -3,6 +3,23 @@
 import jax.numpy as jnp
 from jax import lax
 from jax.sharding import PartitionSpec as P
+
+
+def joined_along(tiles, dim):
+    tiles = jnp.moveaxis(tiles, 0, dim)
+    dims = tiles.shape
+    return tiles.reshape(*dims[:dim], dims[dim] * dims[dim + 1], *dims[dim + 2 :])
+
+
+def gather_around(x, axis, dim):
+    length = lax.axis_size(axis)
+    right = [(i, (i + 1) % length) for i in range(length)]
+    blocks = [x]
+    while len(blocks) < length:
+        blocks.append(lax.ppermute(blocks[-1], axis, right))
+    index = lax.axis_index(axis)
+    blocks = jnp.stack(blocks)[(index - jnp.arange(length)) % length]
+    return joined_along(blocks, dim)
 
 
 def passed_along(array, axis, by):
@@ -46,11 +63,7 @@
     up_low = up_param[0].astype(jnp.bfloat16)
     down_low = down_param[0].astype(jnp.bfloat16)
     columns = normed
-    pre = jnp.dot(
-        columns,
-        lax.all_gather(up_low, "zero", axis=0, tiled=True),
-        preferred_element_type=jnp.float32,
-    )
+    pre = jnp.dot(columns, gather_around(up_low, "zero", 0), preferred_element_type=jnp.float32)
     active, backward = jax.vjp(gelu_tanh, pre)
     act_grad = lax.dot_general(
         grad_rows,

time: 455 us -> 444 us (0.976)
  waiting for transfers between devices: 385 us -> 336 us
  starting transfers between devices: 3.29 us -> 33.3 us
  local copies, waits for them, and re-layouts: 0.02 us -> 7.01 us
  other arithmetic: 27.5 us -> 32.1 us
    ppermute x0 -> x3, waiting for transfers between devices: none -> 109 us  [gather_around(): blocks.append(lax.ppermute(blocks[-1], axis, right))]
    all_gather x1 -> x0, waiting for transfers between devices: 80.4 us -> none  [body(): lax.all_gather(up_low, 'zero', axis=0, tiled=True)]
    all_gather x1, waiting for transfers between devices: 74.8 us -> 0.02 us  [body(): lax.all_gather(down_low, 'zero', axis=0, tiled=True)]
    ppermute x0 -> x3, starting transfers between devices: none -> 30 us  [gather_around(): blocks.append(lax.ppermute(blocks[-1], axis, right))]
    reduce_scatter x1, waiting for transfers between devices: 72.8 us -> 64.2 us  [body(): lax.psum_scatter(across_rows(columns, grad_rows).astype(jnp.bfloat16), 'z...]
    reduce_scatter x1, waiting for transfers between devices: 67.3 us -> 72.9 us  [body(): lax.psum_scatter(across_rows(columns, pre_grad).astype(jnp.bfloat16), 'ze...]
    gather x0 -> x1, local copies, waits for them, and re-layouts: none -> 5.06 us  [gather_around(): blocks = jnp.stack(blocks)[(index - jnp.arange(length)) % length]]
  transfers between devices with their start and end apart: 6 -> 8, of which waited for: 6 -> 7; matrix products, arithmetic and copies ran while one was open for 5% -> 9% of each run, Pallas kernels for 0% -> 0%
where the time goes in v1:
time: 444 us
  waiting for transfers between devices  336 us (76%)
  starting transfers between devices  33.3 us (7%)
  other arithmetic  32.1 us (7%)
  matrix products  20.6 us (5%)
  between operations  14.6 us (3%)
  local copies, waits for them, and re-layouts  7.01 us (2%)
    ppermute x3, waiting for transfers between devices, gather_around(): blocks.append(lax.ppermute(blocks[-1], axis, right))  109 us
    ppermute x2, waiting for transfers between devices, passed_along(): lax.ppermute(array, axis, [(i, (i + by) % size) for i in range(size)])  89.4 us
    reduce_scatter x1, waiting for transfers between devices, body(): lax.psum_scatter(across_rows(columns, pre_grad).astype(jnp.bfloat16), 'ze...  72.9 us
    reduce_scatter x1, waiting for transfers between devices, body(): lax.psum_scatter(across_rows(columns, grad_rows).astype(jnp.bfloat16), 'z...  64.2 us
    ppermute x3, starting transfers between devices, gather_around(): blocks.append(lax.ppermute(blocks[-1], axis, right))  30 us
    dot_general x2, matrix products, across_rows(): lax.dot_general(left, right, (((0,), (0,)), ((), ())), preferred_element_...  16 us
  transfers between devices with their start and end apart: 8, of which 7 were waited for; matrix products, arithmetic and copies ran while one was open for 9% of the time, Pallas kernels for 0%

profile of v1, /device:TPU:0, one launch (start us, length us, event | category | flops | bytes accessed | tf_op | source)
XLA Modules:
  0.0 443.6 jit_solution(2718070982692196620)
XLA Ops:
  7.2 0.0 copy-start
  7.2 0.0 copy-start.2
  7.2 0.0 all-gather.2.cloned.1.call-start
  7.2 2.9 bitcast_convert_fusion
  10.1 0.0 all-gather.2.cloned.1.call-update
  10.1 0.0 reduce-scatter.5.cloned.1.call-start
  10.2 0.0 copy-done.2
  10.2 1.1 fusion.51
  11.3 0.0 copy-start.4
  11.4 3.1 collective-permute-start.6
  14.4 39.8 %collective-permute-done.6 = bf16[256,2048]{1,0:T(8,128)(2,1)S(1)} collective-permute-done((bf16[256,2048]{1,0:T(8,128)(2,1)S(1)}, bf16[256,2048]{1,0:T(8,128)(2,1)S(1)}, u32[]{:S(2)}, u32[]{:S(2)}) %collective-permute-start.6) | collective-permute-done | bytes 1048608 | tf_op jit(solution)/shard_map/ppermute | solution.py:19
  54.2 16.7 %collective-permute-start.7 = (bf16[256,2048]{1,0:T(8,128)(2,1)S(1)}, bf16[256,2048]{1,0:T(8,128)(2,1)}, u32[]{:S(2)}, u32[]{:S(2)}) collective-permute-start(bf16[256,2048]{1,0:T(8,128)(2,1)S(1)} %collective-permute-done.6), channel_id=1, source_target_pairs={{0,1},{1,2},{2,3},{3,0},{4,5},{5,6},{6,7},{7,4},{8,9},{9,10},{10,1... | collective-permute-start | bytes 3145736 | tf_op jit(solution)/shard_map/ppermute | solution.py:19
  70.9 47.1 %collective-permute-done.7 = bf16[256,2048]{1,0:T(8,128)(2,1)} collective-permute-done((bf16[256,2048]{1,0:T(8,128)(2,1)S(1)}, bf16[256,2048]{1,0:T(8,128)(2,1)}, u32[]{:S(2)}, u32[]{:S(2)}) %collective-permute-start.7) | collective-permute-done | bytes 1048608 | tf_op jit(solution)/shard_map/ppermute | solution.py:19
  118.0 10.3 %collective-permute-start.8 = (bf16[256,2048]{1,0:T(8,128)(2,1)}, bf16[256,2048]{1,0:T(8,128)(2,1)}, u32[]{:S(2)}, u32[]{:S(2)}) collective-permute-start(bf16[256,2048]{1,0:T(8,128)(2,1)} %collective-permute-done.7), channel_id=1, source_target_pairs={{0,1},{1,2},{2,3},{3,0},{4,5},{5,6},{6,7},{7,4},{8,9},{9,10},{10,1... | collective-permute-start | bytes 3145736 | tf_op jit(solution)/shard_map/ppermute | solution.py:19
  128.3 1.4 convert_reduce_fusion
  129.8 1.6 fusion.11
  131.4 22.5 %collective-permute-done.8 = bf16[256,2048]{1,0:T(8,128)(2,1)} collective-permute-done((bf16[256,2048]{1,0:T(8,128)(2,1)}, bf16[256,2048]{1,0:T(8,128)(2,1)}, u32[]{:S(2)}, u32[]{:S(2)}) %collective-permute-start.8) | collective-permute-done | bytes 1048608 | tf_op jit(solution)/shard_map/ppermute | solution.py:19
  153.9 0.0 copy-done.4
  153.9 3.4 pad_maximum_fusion
  157.4 0.0 copy-start.3
  157.4 5.1 %gather_fusion = bf16[4,256,2048]{2,1,0:T(8,128)(2,1)} fusion(bf16[4,256,2048]{2,1,0:T(8,128)(2,1)} %pad_maximum_fusion, s32[1024]{0:T(1024)S(1)} %pad_clamp_fusion), kind=kCustom, calls=%fused_computation | custom fusion | bytes 8388624 | tf_op jit(solution)/shard_map/gather | solution.py:21
  162.4 0.0 copy-done.3
  162.4 4.6 %fusion.27 = f32[512,2048]{1,0:T(8,128)S(1)} fusion(bf16[1024,2048]{1,0:T(8,128)(2,1)} %bitcast.78, bf16[1,512,1024]{2,1,0:T(8,128)(2,1)S(1)} %copy-done.3, f32[512]{0:T(512)S(1)} %add_rsqrt_fusion, f32[512]{0:T(512)S(1)} %broadcast_multiply_fusion), kind=kOutput, calls=%fused_computation.48 | convolution fusion | flops 2149580800 | bytes 9441280 | tf_op jit(solution)/shard_map/dot_general | solution.py:66
  167.0 0.0 copy-start.5
  167.1 1.9 copy-done.5
  169.0 0.0 copy-done
  169.0 4.9 %convolution_convert_fusion = bf16[2048,1024]{1,0:T(8,128)(2,1)} fusion(f32[512,2048]{1,0:T(8,128)S(1)} %fusion.27, bf16[1,512,1024]{2,1,0:T(8,128)(2,1)S(1)} %copy-done), kind=kOutput, calls=%fused_computation.13 | convolution fusion | flops 2159017984 | bytes 9437184 | tf_op jit(solution)/shard_map/dot_general | solution.py:46
  173.9 0.0 reduce-scatter.5.cloned.1.call-update
  174.0 0.2 reduce-scatter.3.cloned.1.call-start
  174.2 0.0 all-gather.2.cloned.1.call-done
  174.2 11.1 %convolution_convert_fusion.1 = bf16[1024,2048]{1,0:T(8,128)(2,1)} fusion(f32[512,2048]{1,0:T(8,128)} %copy-done.5, bf16[1,512,1024]{2,1,0:T(8,128)(2,1)S(1)} %copy-done.3, bf16[2048,1024]{1,0:T(8,128)(2,1)} %all-gather.2.cloned.1.call-done, bf16[1,512,1024]{2,1,0:T(8,128)(2,1)S(1)} %copy-done, f32[512]{0:T(512)S(1)} %add_rsqrt_fusion, ...), kind=kOutput, calls=%fused_computation.14 | convolution fusion | flops 4324327424 | bytes 14684160 | tf_op jit(solution)/shard_map/dot_general | solution.py:46
  185.3 0.0 reduce-scatter.3.cloned.1.call-update
  186.1 64.2 %reduce-scatter.5.cloned.1.call-done = bf16[512,1024]{1,0:T(8,128)(2,1)} async-done(((bf16[2048,1024]{1,0:T(8,128)(2,1)}), bf16[512,1024]{1,0:T(8,128)(2,1)}) %reduce-scatter.5.cloned.1.call-update) | async-done | bytes 1048592 | tf_op jit(solution)/shard_map/reduce_scatter | solution.py:81
  250.3 6.7 %fusion.24 = (f32[1,512,1024]{2,1,0:T(8,128)}, f32[512,1024]{1,0:T(8,128)S(1)}, f32[1,512,1024]{2,1,0:T(8,128)}) fusion(bf16[512,1024]{1,0:T(8,128)(2,1)} %reduce-scatter.5.cloned.1.call-done, f32[1,512,1024]{2,1,0:T(8,128)} %param.20, f32[]{:T(128)} %bitcast.13, f32[]{:T(128)} %bitcast.11, f32[1,512,1024]{2,1,0:T(8,128)} %param.18, f32[1,512,1024]{2,1,0:T(8,128)} %param.16), kind=kLoop, calls=%fused_computation.45 | loop fusion | flops 7340032 | bytes 13631496 | tf_op jit(solution)/shard_map/broadcast_in_dim | solution.py:107
  257.0 72.9 %reduce-scatter.3.cloned.1.call-done = bf16[256,2048]{1,0:T(8,128)(2,1)} async-done(((bf16[1024,2048]{1,0:T(8,128)(2,1)}), bf16[256,2048]{1,0:T(8,128)(2,1)}) %reduce-scatter.3.cloned.1.call-update) | async-done | bytes 1048592 | tf_op jit(solution)/shard_map/reduce_scatter | solution.py:77
  329.9 7.4 %fusion.25 = (f32[1,256,2048]{2,1,0:T(8,128)}, f32[256,2048]{1,0:T(8,128)}, f32[1,256,2048]{2,1,0:T(8,128)}) fusion(bf16[256,2048]{1,0:T(8,128)(2,1)} %reduce-scatter.3.cloned.1.call-done, f32[1,256,2048]{2,1,0:T(8,128)} %param.19, f32[]{:T(128)} %bitcast.13, f32[]{:T(128)} %bitcast.11, f32[1,256,2048]{2,1,0:T(8,128)} %param.17, f32[1,256,2048]{2,1,0:T(8,128)} %param.15), kind=kLoop, calls=%fused_computation.46 | loop fusion | flops 7340032 | bytes 13631496 | tf_op jit(solution)/shard_map/broadcast_in_dim | solution.py:106
  337.4 92.3 %conditional.1 = (f32[256,2048]{1,0:T(8,128)}, f32[512,1024]{1,0:T(8,128)}) conditional(s32[]{:T(128)} %clamp.3, (f32[256,2048]{1,0:T(8,128)}, f32[512,1024]{1,0:T(8,128)S(1)}) %tuple.20, (f32[256,2048]{1,0:T(8,128)}, f32[512,1024]{1,0:T(8,128)S(1)}) %tuple.20, (f32[256,2048]{1,0:T(8,128)}, f32[512,1024]{1,0:T(8,128)S(1)}) %tuple.20), branch_computations={%region_4.5_spmd, %region_5.6_spmd, %region_6.7_spmd} | conditional | bytes 16777312 | solution.py:98
  337.4 2.4 collective-permute-start.2
  339.8 0.6 collective-permute-start.3
  340.3 45.9 %collective-permute-done.2 = f32[256,2048]{1,0:T(8,128)} collective-permute-done((f32[256,2048]{1,0:T(8,128)}, f32[256,2048]{1,0:T(8,128)}, u32[]{:S(2)}, u32[]{:S(2)}) %collective-permute-start.2) | collective-permute-done | bytes 2097184 | tf_op jit(solution)/shard_map/cond/branch_1_fun/ppermute | solution.py:27
  386.2 43.5 %collective-permute-done.3 = f32[512,1024]{1,0:T(8,128)} collective-permute-done((f32[512,1024]{1,0:T(8,128)S(1)}, f32[512,1024]{1,0:T(8,128)}, u32[]{:S(2)}, u32[]{:S(2)}) %collective-permute-start.3) | collective-permute-done | bytes 2097184 | tf_op jit(solution)/shard_map/cond/branch_1_fun/ppermute | solution.py:27
  429.7 4.0 multiply_bitcast_fusion.1
  433.7 0.0 copy-start.1
  433.7 3.4 multiply_bitcast_fusion
  437.1 0.0 copy-done.1
  (4 shorter events, 0.0 us)
Async XLA Ops:
  7.2 161.8 %copy-start = (bf16[1,512,1024]{2,1,0:T(8,128)(2,1)S(1)}, bf16[1,512,1024]{2,1,0:T(8,128)(2,1)}, u32[]{:S(2)}) copy-start(bf16[1,512,1024]{2,1,0:T(8,128)(2,1)} %param.13) | copy-start | bytes 3145732
  7.2 3.0 copy-start.2
  7.2 167.0 %all-gather.2.cloned.1.call-start = ((), (), s32[]{:S(2)}) async-start(), calls=%async_computation.2 | async-start | bytes 5242880 | tf_op jit(solution)/shard_map/all_gather | solution.py:70
  10.1 240.1 %reduce-scatter.5.cloned.1.call-start = ((), (), s32[]{:S(2)}) async-start(), calls=%async_computation.4 | async-start | bytes 5242880 | tf_op jit(solution)/shard_map/reduce_scatter | solution.py:81
  11.3 142.6 %copy-start.4 = (bf16[1,256,2048]{2,1,0:T(8,128)(2,1)S(1)}, bf16[1,256,2048]{2,1,0:T(8,128)(2,1)}, u32[]{:S(2)}) copy-start(bf16[1,256,2048]{2,1,0:T(8,128)(2,1)} %get-tuple-element.34) | copy-start | bytes 3145732
  11.4 42.9 %collective-permute-start.6 = (bf16[256,2048]{1,0:T(8,128)(2,1)S(1)}, bf16[256,2048]{1,0:T(8,128)(2,1)S(1)}, u32[]{:S(2)}, u32[]{:S(2)}) collective-permute-start(bf16[256,2048]{1,0:T(8,128)(2,1)S(1)} %get-tuple-element.35), channel_id=1, source_target_pairs={{0,1},{1,2},{2,3},{3,0},{4,5},{5,6},{6,7},{7,4},{8,9},{9,10},{10,1... | collective-permute-start | bytes 3145736 | tf_op jit(solution)/shard_map/ppermute | solution.py:19
  54.2 63.7 %collective-permute-start.7 = (bf16[256,2048]{1,0:T(8,128)(2,1)S(1)}, bf16[256,2048]{1,0:T(8,128)(2,1)}, u32[]{:S(2)}, u32[]{:S(2)}) collective-permute-start(bf16[256,2048]{1,0:T(8,128)(2,1)S(1)} %collective-permute-done.6), channel_id=1, source_target_pairs={{0,1},{1,2},{2,3},{3,0},{4,5},{5,6},{6,7},{7,4},{8,9},{9,10},{10,1... | collective-permute-start | bytes 3145736 | tf_op jit(solution)/shard_map/ppermute | solution.py:19
  118.0 36.0 %collective-permute-start.8 = (bf16[256,2048]{1,0:T(8,128)(2,1)}, bf16[256,2048]{1,0:T(8,128)(2,1)}, u32[]{:S(2)}, u32[]{:S(2)}) collective-permute-start(bf16[256,2048]{1,0:T(8,128)(2,1)} %collective-permute-done.7), channel_id=1, source_target_pairs={{0,1},{1,2},{2,3},{3,0},{4,5},{5,6},{6,7},{7,4},{8,9},{9,10},{10,1... | collective-permute-start | bytes 3145736 | tf_op jit(solution)/shard_map/ppermute | solution.py:19
  157.4 5.1 %copy-start.3 = (bf16[1,512,1024]{2,1,0:T(8,128)(2,1)S(1)}, bf16[1,512,1024]{2,1,0:T(8,128)(2,1)}, u32[]{:S(2)}) copy-start(bf16[1,512,1024]{2,1,0:T(8,128)(2,1)} %param.12) | copy-start | bytes 3145732
  167.0 1.9 copy-start.5
  174.0 156.0 %reduce-scatter.3.cloned.1.call-start = ((), (), s32[]{:S(2)}) async-start(), calls=%async_computation.3 | async-start | bytes 5242880 | tf_op jit(solution)/shard_map/reduce_scatter | solution.py:77
  337.4 48.8 %collective-permute-start.2 = (f32[256,2048]{1,0:T(8,128)}, f32[256,2048]{1,0:T(8,128)}, u32[]{:S(2)}, u32[]{:S(2)}) collective-permute-start(f32[256,2048]{1,0:T(8,128)} %get-tuple-element.14), channel_id=1, source_target_pairs={{0,24},{4,28},{8,0},{12,4},{16,8},{20,12},{24,16},{28,20},{1,25},{... | collective-permute-start | bytes 6291464 | tf_op jit(solution)/shard_map/cond/branch_1_fun/ppermute | solution.py:27
  339.8 89.9 %collective-permute-start.3 = (f32[512,1024]{1,0:T(8,128)S(1)}, f32[512,1024]{1,0:T(8,128)}, u32[]{:S(2)}, u32[]{:S(2)}) collective-permute-start(f32[512,1024]{1,0:T(8,128)S(1)} %get-tuple-element.15), channel_id=1, source_target_pairs={{0,24},{4,28},{8,0},{12,4},{16,8},{20,12},{24,16},{28,20},{1,25},{... | collective-permute-start | bytes 6291464 | tf_op jit(solution)/shard_map/cond/branch_1_fun/ppermute | solution.py:27
  433.7 3.4 copy-start.1
Sparse Core Ops, SparseCore 0:
  10.3 119.7 all-gather.1
  174.1 76.1 reduce-scatter.4
  252.6 77.2 reduce-scatter.2
